TPU v7x, 32 devices: a whole 2x2x4 slice. The times are simulated.
32 devices in a mesh: dp: 4 (over y, x), fsdp: 8 (over z, core).
Axes of the slice: x: 2, y: 2, z: 4, core: 2. Of those that a mesh axis runs over, the one named last changes fastest.
Arguments:
- input_tokens: int32 [2, 32768], P(None, ('dp', 'fsdp')), may hold values from 0 to 29
- item_numbers: int32 [2, 32768], P(None, ('dp', 'fsdp')), may hold values from -1 to 3, as said below
- loss_positions: int32 [2, 4096], P(None, ('dp', 'fsdp')), may hold values from -1 to 1023, as said below
- target_tokens: int32 [2, 4096], P(None, ('dp', 'fsdp')), may hold values from 0 to 29
- input_projection: float32 [1280, 640], P('fsdp', 'dp'), may hold values from -0.15625 to 0.15625
- dilated_conv: float32 [3200, 640], P('fsdp', 'dp'), may hold values from -0.109375 to 0.109375
- output_projection: float32 [1280, 640], P('fsdp', 'dp'), may hold values from -0.25 to 0.25
- vectors: float32 [68, 1280], P(None, ('dp', 'fsdp'))
- input_first_moment: float32 [1280, 640], P('fsdp'), may hold values from -6.67572e-06 to 6.67572e-06
- input_second_moment: float32 [1280, 640], P('fsdp'), may hold values from 5.3002034e-12 to 2.1200814e-11
- conv_first_moment: float32 [3200, 640], P('fsdp'), may hold values from -6.67572e-06 to 6.67572e-06
- conv_second_moment: float32 [3200, 640], P('fsdp'), may hold values from 5.3002034e-12 to 2.1200814e-11
- output_first_moment: float32 [1280, 640], P('fsdp'), may hold values from -6.67572e-06 to 6.67572e-06
- output_second_moment: float32 [1280, 640], P('fsdp'), may hold values from 5.3002034e-12 to 2.1200814e-11
- vector_first_moment: float32 [68, 1280], P(None, ('dp', 'fsdp')), may hold values from -1.9073486e-05 to 1.9073486e-05
- vector_second_moment: float32 [68, 1280], P(None, ('dp', 'fsdp')), may hold values from 4.7701832e-11 to 1.9080733e-10
- bases: float32 [3, 640, 640], replicated, as said below
- eigenbasis_flags: int32 [3], replicated, may hold values from 0 to 1, as said below
- optimizer_step: int32 [1], replicated, may hold values from 2 to 20
Outputs:
- mean_loss: float32 [], replicated
- grad_norm: float32 [], replicated
- master_in: float32 [1280, 640], P('fsdp', 'dp')
- copy_in: bfloat16 [1280, 640], P('fsdp', 'dp')
- moment_in: float32 [1280, 640], P('fsdp')
- square_in: float32 [1280, 640], P('fsdp')
- updated_conv: float32 [3200, 640], P('fsdp', 'dp')
- conv_bfloat_copy: bfloat16 [3200, 640], P('fsdp', 'dp')
- updated_conv_moment: float32 [3200, 640], P('fsdp')
- updated_conv_square: float32 [3200, 640], P('fsdp')
- master_out: float32 [1280, 640], P('fsdp', 'dp')
- copy_out: bfloat16 [1280, 640], P('fsdp', 'dp')
- moment_out: float32 [1280, 640], P('fsdp')
- square_out: float32 [1280, 640], P('fsdp')
- master_vec: float32 [68, 1280], P(None, ('dp', 'fsdp'))
- copy_vec: bfloat16 [68, 1280], P(None, ('dp', 'fsdp'))
- moment_vec: float32 [68, 1280], P(None, ('dp', 'fsdp'))
- square_vec: float32 [68, 1280], P(None, ('dp', 'fsdp'))
Inputs may be any that keep to these rules, and one draw needn't show every extreme that they name: `item_numbers`: each device's 1024 slots of a micro-batch hold whole items of 256, 512 or 1024 tokens, numbered from 0 in order and starting at slot 0, followed by padding marked -1; items fill at least half of the slots; some device holds one item of 1024 tokens. `loss_positions`: slot i of a device's 128 slots in a micro-batch holds -1 or a position from 8 i to 8 i + 7 of that device's slots; it holds a position exactly when that position belongs to an item. `eigenbasis_flags`: two of the three entries are 1. `bases`: each matrix is orthogonal.
All inputs are finite; a program needn't handle non-finite values.
Results may differ from a plain program's by a relative error of at most 0.0091.
Values may be sent and summed in bfloat16 or wider, within the bound.
A program may use at most 256 MiB of HBM per device.

v0:
```python
from functools import partial

import jax
import jax.numpy as jnp
from jax import lax
from jax.sharding import PartitionSpec as P

VOCAB = 30
CONV_TAPS = 5
DILATION = 8


beta_one = 0.9
beta_two = 0.95
epsilon = 1e-08
rate_matrix = 0.02
rate_vector = 0.5
decay_weight = 0.01
clip_limit = 0.02
norm_eps = 1e-05
highest_precision = lax.Precision.HIGHEST


def layer_norm(values, norm_gain, norm_bias):
    centre = values - jnp.mean(values, axis=-1, keepdims=True)
    spread = jnp.mean(centre * centre, axis=-1, keepdims=True)
    return centre * lax.rsqrt(spread + norm_eps) * norm_gain + norm_bias


def norm_gelu(values, norm_gain, norm_bias):
    return jax.nn.gelu(layer_norm(values, norm_gain, norm_bias), approximate=True)


def shifted(values, offset, filler):
    if offset > 0:
        pad_rows = jnp.full((offset,) + values.shape[1:], filler, values.dtype)
        return jnp.concatenate([values[offset:], pad_rows], axis=0)
    if offset < 0:
        pad_rows = jnp.full((-offset,) + values.shape[1:], filler, values.dtype)
        return jnp.concatenate([pad_rows, values[:offset]], axis=0)
    return values


def build_masks(item_row):
    result = []
    for tap_index in range(CONV_TAPS):
        offset = (tap_index - CONV_TAPS // 2) * DILATION
        same_item = (shifted(item_row, offset, -2) == item_row) & (item_row >= 0)
        result.append((offset, same_item))
    return result


def unfold(values, masks):
    return jnp.concatenate(
        [
            shifted(values, offset, 0) * same_item[:, None].astype(values.dtype)
            for offset, same_item in masks
        ],
        axis=1,
    )


def fold_columns(column_gradient, masks, inner_width):
    total = jnp.zeros((column_gradient.shape[0], inner_width), jnp.float32)
    for tap_index in range(len(masks)):
        offset, same_item = masks[tap_index]
        piece = column_gradient[
            :, tap_index * inner_width : (tap_index + 1) * inner_width
        ] * same_item[:, None].astype(jnp.float32)
        total = total + shifted(piece, -offset, 0.0)
    return total


def slot_loss(logits, labels, valid_slot):
    log_total = jax.nn.logsumexp(logits, axis=-1)
    hits = labels[:, None] == jnp.arange(logits.shape[1], dtype=jnp.int32)[None, :]
    chosen = jnp.sum(jnp.where(hits, logits, 0.0), axis=-1)
    return jnp.sum(jnp.where(valid_slot, log_total - chosen, 0.0))


def column_sum(values):
    return jnp.sum(values, axis=0, dtype=jnp.float32)


def gathered_weights(shards):
    parted = (
        lax.all_gather(shards[0], "fsdp", axis=0, tiled=True),
        lax.all_gather(shards[1], "fsdp", axis=0, tiled=True),
        lax.all_gather(shards[2], "fsdp", axis=0, tiled=True),
        lax.all_gather(shards[3], "fsdp", axis=1, tiled=True),
    )
    return (
        lax.all_gather(parted[0], "dp", axis=1, tiled=True),
        lax.all_gather(parted[1], "dp", axis=1, tiled=True),
        lax.all_gather(parted[2], "dp", axis=1, tiled=True),
        lax.all_gather(parted[3], "dp", axis=1, tiled=True),
    )


def forward(weight_list, tokens, item_row, slot_list, targets):
    input_projection, dilated_conv, output_projection, embedding_bfloat = weight_list
    embedding_table = embedding_bfloat.astype(jnp.float32)
    inner_width = input_projection.shape[1]
    starting_row = 2 * VOCAB
    onehot = (tokens[:, None] == jnp.arange(VOCAB, dtype=jnp.int32)[None, :]).astype(jnp.bfloat16)
    embedded = jnp.dot(onehot, embedding_bfloat[:VOCAB], preferred_element_type=jnp.float32)
    first_act, first_back = jax.vjp(
        norm_gelu, embedded, embedding_table[starting_row], embedding_table[starting_row + 1]
    )
    first_low = first_act.astype(jnp.bfloat16)
    pre_inner = (
        jnp.dot(first_low, input_projection, preferred_element_type=jnp.float32)
        + embedding_table[starting_row + 6, :inner_width]
    )
    second_act, second_back = jax.vjp(
        norm_gelu,
        pre_inner,
        embedding_table[starting_row + 5, :inner_width],
        embedding_table[starting_row + 5, inner_width:],
    )
    masks = build_masks(item_row)
    column_list = unfold(second_act.astype(jnp.bfloat16), masks)
    conv_input = (
        jnp.dot(column_list, dilated_conv, preferred_element_type=jnp.float32)
        + embedding_table[starting_row + 6, inner_width:]
    )
    third_act, third_back = jax.vjp(
        norm_gelu,
        conv_input,
        embedding_table[starting_row + 7, :inner_width],
        embedding_table[starting_row + 7, inner_width:],
    )
    third_low = third_act.astype(jnp.bfloat16)
    branch = (
        jnp.einsum("ti,di->td", third_low, output_projection, preferred_element_type=jnp.float32)
        + embedding_table[starting_row + 2]
    )
    final_out, final_back = jax.vjp(
        layer_norm,
        embedded + branch,
        embedding_table[starting_row + 3],
        embedding_table[starting_row + 4],
    )
    safe_slots = jnp.maximum(slot_list, 0)
    picked = final_out[safe_slots].astype(jnp.bfloat16)
    logits = jnp.einsum(
        "pd,vd->pv",
        picked,
        embedding_bfloat[VOCAB:starting_row],
        preferred_element_type=jnp.float32,
    )
    loss_part, loss_back = jax.vjp(
        partial(slot_loss, labels=targets, valid_slot=slot_list >= 0), logits
    )
    kept_state = (
        onehot,
        first_back,
        first_low,
        second_back,
        masks,
        column_list,
        third_back,
        third_low,
        final_back,
        safe_slots,
        picked,
        loss_back,
    )
    return (kept_state, loss_part)


def backward(weight_list, kept_state):
    input_projection, dilated_conv, output_projection, embedding_bfloat = weight_list
    (
        onehot,
        first_back,
        first_low,
        second_back,
        masks,
        column_list,
        third_back,
        third_low,
        final_back,
        safe_slots,
        picked,
        loss_back,
    ) = kept_state
    inner_width = input_projection.shape[1]
    starting_row = 2 * VOCAB
    logit_grad = loss_back(jnp.ones((), jnp.float32))[0].astype(jnp.bfloat16)
    head_grad = jnp.einsum("pv,pd->vd", logit_grad, picked, preferred_element_type=jnp.float32)
    picked_grad = jnp.einsum(
        "pv,vd->pd",
        logit_grad,
        embedding_bfloat[VOCAB:starting_row],
        preferred_element_type=jnp.float32,
    )
    final_grad = (
        jnp.zeros((onehot.shape[0], picked.shape[1]), jnp.float32).at[safe_slots].add(picked_grad)
    )
    sum_grad, gain_four, bias_four = final_back(final_grad)
    branch_low = sum_grad.astype(jnp.bfloat16)
    out_grad = jnp.einsum("td,ti->di", branch_low, third_low, preferred_element_type=jnp.float32)
    third_grad = jnp.einsum(
        "td,di->ti", branch_low, output_projection, preferred_element_type=jnp.float32
    )
    conv_pre, gain_three, bias_three = third_back(third_grad)
    conv_bfloat = conv_pre.astype(jnp.bfloat16)
    conv_grad = jnp.einsum(
        "tk,ti->ki", column_list, conv_bfloat, preferred_element_type=jnp.float32
    )
    column_gradient = jnp.einsum(
        "le,de->ld", conv_bfloat, dilated_conv, preferred_element_type=jnp.float32
    )
    second_grad = fold_columns(column_gradient, masks, inner_width)
    inner_pre, gain_two, bias_two = second_back(second_grad)
    inner_low = inner_pre.astype(jnp.bfloat16)
    in_grad = jnp.einsum("td,ti->di", first_low, inner_low, preferred_element_type=jnp.float32)
    first_grad = jnp.einsum(
        "ti,di->td", inner_low, input_projection, preferred_element_type=jnp.float32
    )
    start_grad, gain_one, bias_one = first_back(first_grad)
    start_grad = start_grad + sum_grad
    table_grad = jnp.einsum(
        "tv,td->vd", onehot.astype(jnp.float32), start_grad, precision=highest_precision
    )
    small_rows = jnp.stack(
        [
            gain_one,
            bias_one,
            column_sum(branch_low),
            gain_four,
            bias_four,
            jnp.concatenate([gain_two, bias_two]),
            jnp.concatenate([column_sum(inner_low), column_sum(conv_bfloat)]),
            jnp.concatenate([gain_three, bias_three]),
        ]
    )
    vec_grad = jnp.concatenate([table_grad, head_grad, small_rows], axis=0)
    return (in_grad, conv_grad, out_grad, vec_grad)


def eigenbasis_update(
    gradient, master, moment, square, rotated_grads, col_start, first_correction, second_correction
):
    rotated = jnp.dot(gradient, rotated_grads, precision=highest_precision)
    moment_new = beta_one * moment + (1.0 - beta_one) * rotated
    square_new = beta_two * square + (1.0 - beta_two) * rotated * rotated
    step_ratio = (
        moment_new / first_correction / (jnp.sqrt(square_new / second_correction) + epsilon)
    )
    own_basis = lax.dynamic_slice_in_dim(rotated_grads, col_start, master.shape[1], 0)
    update = jnp.einsum("ri,ci->rc", step_ratio, own_basis, precision=highest_precision)
    master_new = master - rate_matrix * (update + decay_weight * master)
    return (master_new, master_new.astype(jnp.bfloat16), moment_new, square_new)


def adam_vectors(gradient, master, moment, square, first_correction, second_correction):
    decay_rows = jnp.where(
        jnp.arange(master.shape[0], dtype=jnp.int32)[:, None] < 2 * VOCAB, decay_weight, 0.0
    )
    moment_new = beta_one * moment + (1.0 - beta_one) * gradient
    square_new = beta_two * square + (1.0 - beta_two) * gradient * gradient
    step_ratio = (
        moment_new / first_correction / (jnp.sqrt(square_new / second_correction) + epsilon)
    )
    master_new = master - rate_vector * (step_ratio + decay_rows * master)
    return (master_new, master_new.astype(jnp.bfloat16), moment_new, square_new)


def local(
    input_tokens,
    item_numbers,
    loss_positions,
    target_tokens,
    input_projection,
    dilated_conv,
    output_projection,
    vectors,
    input_first_moment,
    input_second_moment,
    conv_first_moment,
    conv_second_moment,
    output_first_moment,
    output_second_moment,
    vector_first_moment,
    vector_second_moment,
    bases,
    eigenbasis_flags,
    optimizer_step,
):
    shards_low = (
        input_projection.astype(jnp.bfloat16),
        dilated_conv.astype(jnp.bfloat16),
        output_projection.astype(jnp.bfloat16),
        vectors.astype(jnp.bfloat16),
    )
    grad_sums = None
    summed_loss = jnp.zeros((), jnp.float32)
    for batch_index in range(input_tokens.shape[0]):
        weight_list = gathered_weights(shards_low)
        kept_state, loss_part = forward(
            weight_list,
            input_tokens[batch_index],
            item_numbers[batch_index],
            loss_positions[batch_index],
            target_tokens[batch_index],
        )
        weight_list = gathered_weights(shards_low)
        gradients = backward(weight_list, kept_state)
        summed_loss = summed_loss + loss_part
        grad_sums = (
            gradients
            if grad_sums is None
            else tuple((earlier + current for earlier, current in zip(grad_sums, gradients)))
        )
    groups = lax.axis_size("dp")
    col_index = lax.axis_index("dp")
    in_sum, conv_sum, out_sum, vec_sum = grad_sums
    vec_split = vec_sum.reshape(vec_sum.shape[0], groups, vec_sum.shape[1] // groups)
    in_rows, conv_rows, out_rows, vec_rows = (
        lax.psum_scatter(
            in_sum.astype(jnp.bfloat16), "fsdp", scatter_dimension=0, tiled=True
        ).astype(jnp.float32),
        lax.psum_scatter(
            conv_sum.astype(jnp.bfloat16), "fsdp", scatter_dimension=0, tiled=True
        ).astype(jnp.float32),
        lax.psum_scatter(
            out_sum.astype(jnp.bfloat16), "fsdp", scatter_dimension=0, tiled=True
        ).astype(jnp.float32),
        lax.psum_scatter(
            vec_split.astype(jnp.bfloat16), "fsdp", scatter_dimension=2, tiled=True
        ).astype(jnp.float32),
    )
    in_rows, conv_rows, out_rows, vec_rows = lax.psum(
        (in_rows, conv_rows, out_rows, vec_rows), "dp"
    )
    vec_own = lax.dynamic_index_in_dim(vec_rows, col_index, axis=1, keepdims=False)
    col_width = input_projection.shape[1]
    col_start = col_index * col_width
    owned = [
        lax.dynamic_slice_in_dim(full_rows, col_start, col_width, 1)
        for full_rows in (in_rows, conv_rows, out_rows)
    ]
    square_local = sum((jnp.sum(piece * piece) for piece in owned)) + jnp.sum(vec_own * vec_own)
    slot_count = jnp.sum((loss_positions >= 0).astype(jnp.float32))
    loss_total, count_total, square_total = lax.psum(
        (summed_loss, slot_count, square_local), ("dp", "fsdp")
    )
    grad_norm = jnp.sqrt(square_total) / count_total
    factor = jnp.minimum(1.0, clip_limit / grad_norm) / count_total
    step_value = optimizer_step[0].astype(jnp.float32)
    first_correction = 1.0 - beta_one**step_value
    second_correction = 1.0 - beta_two**step_value
    identity = jnp.eye(bases.shape[1], dtype=jnp.float32)
    rotated_grads = [
        jnp.where(eigenbasis_flags[mat_index] == 1, bases[mat_index], identity)
        for mat_index in range(3)
    ]
    master_in, copy_in, moment_in, square_in = eigenbasis_update(
        in_rows * factor,
        input_projection,
        input_first_moment,
        input_second_moment,
        rotated_grads[0],
        col_start,
        first_correction,
        second_correction,
    )
    updated_conv, conv_bfloat_copy, updated_conv_moment, updated_conv_square = eigenbasis_update(
        conv_rows * factor,
        dilated_conv,
        conv_first_moment,
        conv_second_moment,
        rotated_grads[1],
        col_start,
        first_correction,
        second_correction,
    )
    master_out, copy_out, moment_out, square_out = eigenbasis_update(
        out_rows * factor,
        output_projection,
        output_first_moment,
        output_second_moment,
        rotated_grads[2],
        col_start,
        first_correction,
        second_correction,
    )
    master_vec, copy_vec, moment_vec, square_vec = adam_vectors(
        vec_own * factor,
        vectors,
        vector_first_moment,
        vector_second_moment,
        first_correction,
        second_correction,
    )
    return (
        loss_total / count_total,
        grad_norm,
        master_in,
        copy_in,
        moment_in,
        square_in,
        updated_conv,
        conv_bfloat_copy,
        updated_conv_moment,
        updated_conv_square,
        master_out,
        copy_out,
        moment_out,
        square_out,
        master_vec,
        copy_vec,
        moment_vec,
        square_vec,
    )


def solution(mesh):
    placed = (
        P(None, ("dp", "fsdp")),
        P(None, ("dp", "fsdp")),
        P(None, ("dp", "fsdp")),
        P(None, ("dp", "fsdp")),
        P("fsdp", "dp"),
        P("fsdp", "dp"),
        P("fsdp", "dp"),
        P(None, ("dp", "fsdp")),
        P("fsdp", None),
        P("fsdp", None),
        P("fsdp", None),
        P("fsdp", None),
        P("fsdp", None),
        P("fsdp", None),
        P(None, ("dp", "fsdp")),
        P(None, ("dp", "fsdp")),
        P(),
        P(),
        P(),
    )
    return jax.shard_map(
        local,
        mesh=mesh,
        in_specs=placed,
        out_specs=(
            P(),
            P(),
            P("fsdp", "dp"),
            P("fsdp", "dp"),
            P("fsdp", None),
            P("fsdp", None),
            P("fsdp", "dp"),
            P("fsdp", "dp"),
            P("fsdp", None),
            P("fsdp", None),
            P("fsdp", "dp"),
            P("fsdp", "dp"),
            P("fsdp", None),
            P("fsdp", None),
            P(None, ("dp", "fsdp")),
            P(None, ("dp", "fsdp")),
            P(None, ("dp", "fsdp")),
            P(None, ("dp", "fsdp")),
        ),
        check_vma=False,
    )
```

profile of v0, /device:TPU:0, one launch (start us, length us, event | category | flops | bytes accessed | tf_op | source)
XLA Modules:
  0.0 701.5 jit_solution(10679068037449267303)
XLA Ops:
  8.2 17.0 %all_gather.18 = bf16[1280,160]{1,0:T(8,128)(2,1)S(1)} all-gather(bf16[160,160]{1,0:T(8,128)(2,1)S(1)} %convert_element_type.235), channel_id=1, replica_groups=mesh['dp'=4,'fsdp'=8] {'fsdp'}, dimensions={0}, use_global_device_ids=true | all-gather | bytes 460800 | tf_op jit(solution)/shard_map/all_gather | solution.py:87
  26.2 19.0 %all-gather.1 = bf16[8,400,160]{1,2,0:T(8,128)(2,1)S(1)} all-gather(bf16[1,400,160]{1,2,0:T(8,128)(2,1)S(1)} %convert_bitcast_fusion), channel_id=1, replica_groups=mesh['dp'=4,'fsdp'=8] {'fsdp'}, dimensions={0}, use_global_device_ids=true | all-gather | bytes 1152000 | tf_op jit(solution)/shard_map/all_gather | solution.py:88
  46.0 2.4 reshape.481
  48.5 15.1 %all_gather.22 = bf16[1280,160]{1,0:T(8,128)(2,1)S(1)} all-gather(bf16[160,160]{1,0:T(8,128)(2,1)S(1)} %convert_element_type.244), channel_id=1, replica_groups=mesh['dp'=4,'fsdp'=8] {'fsdp'}, dimensions={0}, use_global_device_ids=true | all-gather | bytes 460800 | tf_op jit(solution)/shard_map/all_gather | solution.py:89
  64.9 14.0 %all_gather.16 = bf16[68,320]{0,1:T(8,128)(2,1)S(1)} all-gather(bf16[68,40]{0,1:T(8,128)(2,1)S(1)} %convert_element_type.232), channel_id=1, replica_groups=mesh['dp'=4,'fsdp'=8] {'fsdp'}, dimensions={1}, use_global_device_ids=true | all-gather | bytes 48960 | tf_op jit(solution)/shard_map/all_gather | solution.py:90
  79.0 8.9 %all-gather = bf16[4,320,68]{1,2,0:T(8,128)(2,1)S(1)} all-gather(bf16[1,320,68]{1,2,0:T(8,128)(2,1)S(1)} %copy.120), channel_id=1, replica_groups=mesh['dp'=4,'fsdp'=8] {'dp'}, dimensions={0}, use_global_device_ids=true | all-gather | bytes 217600 | tf_op jit(solution)/shard_map/all_gather | solution.py:96
  97.3 6.1 multiply_convert_fusion.1
  103.4 5.4 fusion.220
  108.9 2.4 add_reduce_fusion.1
  113.0 2.9 multiply_convert_fusion.5
  127.6 9.4 %fusion.221 = f32[1024,640]{1,0:T(8,128)S(1)} fusion(bf16[1024,3200]{1,0:T(8,128)(2,1)} %multiply_dynamic-update-slice_fusion.5, bf16[3200,640]{0,1:T(8,128)(2,1)} %all-gather.8.cloned.1.call-done), kind=kOutput, calls=%fused_computation.423 | convolution fusion | flops 4194304000 | bytes 13271040 | tf_op jit(solution)/shard_map/dot_general | solution.py:124
  137.0 5.6 add_reduce_fusion
  144.1 2.8 all-gather.10.cloned.1.call-done
  146.9 7.3 %fusion.213 = (f32[1024]{0:T(1024)S(1)}, f32[1024,1280]{1,0:T(8,128)S(1)}) fusion(f32[1024,1280]{1,0:T(8,128)} %copy-done.1, f32[1280]{0:T(1024)S(1)} %get-tuple-element.44, bf16[1280,640]{0,1:T(8,128)(2,1)} %all-gather.10.cloned.1.call-done, f32[640]{0:T(1024)S(1)} %get-tuple-element.48, f32[640]{0:T(1024)S(1)} %get-tuple-element.49, ...), kind=kOutput, calls=%fused_computation.415 | convolution fusion | flops 1690827776 | bytes 14770688 | tf_op jit(solution)/shard_map/ti,di->td/dot_general | solution.py:135
  155.0 2.9 copy-done.13
  158.4 3.4 fusion.214
  164.1 3.1 multiply_add_fusion.2
  167.2 3.2 gather_fusion
  180.1 4.5 scatter_custom_fusion
  184.7 4.4 scatter_custom_fusion.1
  189.1 8.8 %multiply_reduce_fusion.3 = (f32[1280]{0:T(1024)S(1)}, f32[1024]{0:T(1024)S(1)}, f32[1280]{0:T(1024)S(1)}, f32[1280]{0:T(1024)S(1)}, f32[1024]{0:T(1024)S(1)}, /*index=5*/f32[1280]{0:T(1024)S(1)}) fusion(f32[1024,1280]{1,0:T(8,128)} %scatter_custom_fusion, f32[1024,1280]{1,0:T(8,128)} %copy-done.2, f32[1024]{0:T(1024)S(1)} %fusion.142, ...), kind=kLoop, calls=%fused_computation.32 | loop fusion | flops 20964352 | bytes 21021696 | tf_op jit(solution)/shard_map/transpose(jvp())/reduce_sum | solution.py:27
  200.4 8.1 %fusion.199 = (f32[1024]{0:T(1024)S(1)}, f32[1024,1280]{1,0:T(8,128)}, f32[1024]{0:T(1024)S(1)}, f32[1024,1280]{1,0:T(8,128)}) fusion(f32[1024]{0:T(1024)S(1)} %multiply_multiply_fusion.23, f32[1024,1280]{1,0:T(8,128)S(1)} %bitcast.126, f32[1024]{0:T(1024)S(1)} %broadcast_multiply_fusion.6, f32[1024]{0:T(1024)S(1)} %fusion.142, ...), kind=kLoop, calls=%fused_computation.401 | loop fusion | flops 18348032 | bytes 31495168 | tf_op jit(solution)/shard_map/transpose(jvp())/reduce_sum | solution.py:25
  213.8 4.5 convert_reduce_fusion
  219.6 4.6 convert_reduce_fusion.1
  225.6 6.3 fusion.170
  231.9 2.2 fusion.222
  235.2 6.1 multiply_reduce_fusion.17
  241.4 3.2 multiply_reduce_fusion.14
  247.3 6.3 convert_reduce_fusion.4
  254.7 5.4 fusion.223
  260.1 4.2 fusion.200
  264.3 3.7 copy-done.19
  268.0 7.6 %fusion.225 = f32[1024,3200]{1,0:T(8,128)S(1)} fusion(bf16[1024,640]{1,0:T(8,128)(2,1)S(1)} %copy-done.36, bf16[3200,640]{0,1:T(8,128)(2,1)} %all-gather.8.cloned.1.call-done), kind=kOutput, calls=%fused_computation.427 | convolution fusion | flops 4194304000 | bytes 18513920 | tf_op jit(solution)/shard_map/le,de->ld/dot_general | solution.py:212
  275.6 4.3 fusion.201
  279.9 3.5 copy-done.20
  283.5 2.1 slice_multiply_fusion.9
  294.4 8.7 %multiply_reduce_fusion.16 = (f32[1024]{0:T(1024)S(1)}, f32[1024]{0:T(1024)S(1)}, f32[1024,640]{1,0:T(8,128)S(1)}, f32[1024,640]{1,0:T(8,128)S(1)}) fusion(f32[640]{0:T(1024)S(1)} %get-tuple-element.51, f32[1024]{0:T(1024)S(1)} %broadcast_multiply_fusion.1, f32[1024,640]{1,0:T(8,128)S(1)} %copy-done.5, f32[640]{0:T(1024)S(1)} %get-tuple-element.52, ...), kind=kLoop, calls=%fused_computation.119 | loop fusion | flops 41940992 | bytes 36494848 | tf_op jit(solution)/shard_map/transpose(jvp())/reduce_sum | solution.py:27
  303.2 3.2 multiply_reduce_fusion.15
  307.8 6.4 convert_reduce_fusion.3
  318.3 4.2 fusion.227
  322.6 15.2 %multiply_reduce_fusion.1 = (f32[1280]{0:T(1024)S(1)}, f32[1024]{0:T(1024)S(1)}, f32[1280]{0:T(1024)S(1)}, f32[1024,1280]{1,0:T(8,128)S(1)}, f32[1280]{0:T(1024)...) fusion(f32[1024,1280]{1,0:T(8,128)} %copy-done, f32[1024]{0:T(1024)S(1)} %copy-done.91, ...), kind=kOutput, calls=%fused_computation.27 | convolution fusion | flops 1753736192 | bytes 29218816 | tf_op jit(solution)/shard_map/ti,di->td/dot_general | solution.py:219
  337.9 5.7 fusion.174
  348.9 8.9 %fusion.12 = f32[30,1280]{0,1:T(8,128)S(1)} fusion(f32[1024,1280]{1,0:T(8,128)} %get-tuple-element.95, f32[1024,1280]{1,0:T(8,128)} %get-tuple-element.172, f32[1024]{0:T(1024)S(1)} %negate_multiply_fusion, f32[1024]{0:T(1024)S(1)} %negate_multiply_fusion.4, s32[1024]{0:T(1024)S(1)} %bitcast.143), kind=kOutput, calls=%fused_computation.28 | convolution fusion | flops 475822080 | bytes 10651648 | tf_op jit(solution)/shard_map/concatenate | solution.py:239
  357.9 7.3 %fusion.15 = f32[30,1280]{0,1:T(8,128)S(1)} fusion(f32[1024,1280]{1,0:T(8,128)S(1)} %bitcast.128, f32[1024,1280]{1,0:T(8,128)} %get-tuple-element.129, f32[1024]{0:T(1024)S(1)} %negate_multiply_fusion.1, f32[1024]{0:T(1024)S(1)} %negate_multiply_fusion.7, s32[1024]{0:T(1024)S(1)} %bitcast.141), kind=kOutput, calls=%fused_computation.35 | convolution fusion | flops 475822080 | bytes 10651648 | tf_op jit(solution)/shard_map/concatenate | solution.py:239
  365.2 5.0 concatenate.197
  370.2 5.3 concatenate.183
  375.4 2.1 add_convert_fusion.7
  377.8 6.6 fusion.21
  384.5 4.5 fusion.224
  389.0 3.5 fusion.20
  392.6 8.2 %fusion.226 = f32[3200,640]{1,0:T(8,128)S(1)} fusion(bf16[1024,3200]{1,0:T(8,128)(2,1)} %multiply_dynamic-update-slice_fusion.5, bf16[1024,640]{1,0:T(8,128)(2,1)} %copy-done.38), kind=kOutput, calls=%fused_computation.428 | convolution fusion | flops 4194304000 | bytes 16056320 | tf_op jit(solution)/shard_map/tk,ti->ki/dot_general | solution.py:209
  400.9 9.8 %add_convert_fusion = bf16[3200,640]{1,0:T(8,128)(2,1)} fusion(f32[3200,640]{1,0:T(8,128)S(1)} %fusion.226, bf16[1024,3200]{1,0:T(8,128)(2,1)} %copy-done.54, bf16[1024,640]{1,0:T(8,128)(2,1)S(1)} %copy-done.37), kind=kOutput, calls=%fused_computation.4 | convolution fusion | flops 4198400000 | bytes 20152320 | tf_op jit(solution)/shard_map/tk,ti->ki/dot_general | solution.py:209
  415.9 3.9 convert_select_fusion
  421.1 12.3 %all-reduce.30.cloned.1.call-done = bf16[68,4,320]{0,2,1:T(8,128)(2,1)} async-done(((bf16[68,4,320]{0,2,1:T(8,128)(2,1)}), bf16[68,4,320]{0,2,1:T(8,128)(2,1)}) %all-reduce.30.cloned.1.call-update) | async-done | bytes 174096
  434.2 34.9 %reduce-scatter.9.cloned.1.call-done = bf16[160,640]{1,0:T(8,128)(2,1)} async-done(((bf16[1280,640]{1,0:T(8,128)(2,1)}), bf16[160,640]{1,0:T(8,128)(2,1)}) %reduce-scatter.9.cloned.1.call-update) | async-done | bytes 204816 | tf_op jit(solution)/shard_map/reduce_scatter | solution.py:328
  469.1 34.9 %reduce-scatter.5.cloned.1.call-done = bf16[160,640]{1,0:T(8,128)(2,1)} async-done(((bf16[1280,640]{1,0:T(8,128)(2,1)}), bf16[160,640]{1,0:T(8,128)(2,1)}) %reduce-scatter.5.cloned.1.call-update) | async-done | bytes 204816 | tf_op jit(solution)/shard_map/reduce_scatter | solution.py:322
  504.0 49.9 %reduce-scatter.7.cloned.1.call-done = bf16[400,640]{1,0:T(8,128)(2,1)} async-done(((bf16[3200,640]{1,0:T(8,128)(2,1)}), bf16[400,640]{1,0:T(8,128)(2,1)}) %reduce-scatter.7.cloned.1.call-update) | async-done | bytes 512016 | tf_op jit(solution)/shard_map/reduce_scatter | solution.py:325
  553.9 67.4 %all-reduce.31 = (f32[160,640]{1,0:T(8,128)}, f32[400,640]{1,0:T(8,128)}, f32[160,640]{1,0:T(8,128)}, f32[68,4,40]{0,2,1:T(8,128)S(1)}) all-reduce(bf16[160,640]{1,0:T(8,128)(2,1)} %reduce-scatter.5.cloned.1.call-done, bf16[400,640]{1,0:T(8,128)(2,1)} %reduce-scatter.7.cloned.1.call-done, ...), channel_id=1, replica_groups=mesh['dp'=4,'fsdp'=8] {'dp'}, use_global_device_ids=true, to_apply=%region_42.43 | all-reduce | flops 471680 | bytes 2851840 | tf_op jit(solution)/shard_map/psum | solution.py:335
  623.0 1.9 multiply_reduce_fusion.24
  629.7 42.8 %all-reduce.25 = (f32[]{:T(128)}, f32[]{:T(128)}, f32[]{:T(128)}) all-reduce(f32[]{:T(128)S(6)} %add.497, f32[]{:T(128)} %fusion.154, f32[]{:T(128)S(6)} %add.516), channel_id=1, replica_groups=mesh['dp'=4,'fsdp'=8] {'dp','fsdp'}, use_global_device_ids=true, to_apply=%region_24.25 | all-reduce | flops 3 | bytes 24 | tf_op jit(solution)/shard_map/psum | solution.py:347
  676.6 3.2 fusion.81
  681.4 2.8 fusion.219
  685.6 3.2 fusion.66
  688.9 2.4 fusion.218
  (426 shorter events, 86.4 us)
Async XLA Ops:
  7.2 19.0 %copy-start.52 = (f32[400,160]{0,1:T(8,128)S(1)}, f32[400,160]{0,1:T(8,128)}, u32[]{:S(2)}) copy-start(f32[400,160]{0,1:T(8,128)} %param.24) | copy-start | bytes 768004
  7.2 96.2 %all-gather.6.cloned.1.call-start = ((), (), s32[]{:S(2)}) async-start(), calls=%async_computation.3 | async-start | bytes 2048000 | tf_op jit(solution)/shard_map/all_gather | solution.py:93
  26.2 101.4 %all-gather.8.cloned.1.call-start = ((), (), s32[]{:S(2)}) async-start(), calls=%async_computation.4 | async-start | bytes 5120000 | tf_op jit(solution)/shard_map/all_gather | solution.py:94
  46.0 18.7 %copy-start.56 = (s32[2,1024]{1,0:T(2,128)S(1)}, s32[2,1024]{1,0:T(2,128)}, u32[]{:S(2)}) copy-start(s32[2,1024]{1,0:T(2,128)} %param.20) | copy-start | bytes 24580
  46.0 18.9 %copy-start.60 = (f32[68,40]{0,1:T(8,128)S(1)}, f32[68,40]{0,1:T(8,128)}, u32[]{:S(2)}) copy-start(f32[68,40]{0,1:T(8,128)} %param.26) | copy-start | bytes 32644
  48.4 39.9 %copy-start.116 = (s32[2,128]{1,0:T(2,128)S(1)}, s32[2,128]{1,0:T(2,128)}, u32[]{:S(2)}) copy-start(s32[2,128]{1,0:T(2,128)} %param.22) | copy-start | bytes 3076
  48.4 40.5 %copy-start.112 = (s32[2,128]{1,0:T(2,128)S(1)}, s32[2,128]{1,0:T(2,128)}, u32[]{:S(2)}) copy-start(s32[2,128]{1,0:T(2,128)} %param.21) | copy-start | bytes 3076
  48.4 40.5 %copy-start.106 = (s32[2,1024]{1,0:T(2,128)S(1)}, s32[2,1024]{1,0:T(2,128)}, u32[]{:S(2)}) copy-start(s32[2,1024]{1,0:T(2,128)} %param.19) | copy-start | bytes 24580
  48.5 98.4 %all-gather.10.cloned.1.call-start = ((), (), s32[]{:S(2)}) async-start(), calls=%async_computation.5 | async-start | bytes 2048000 | tf_op jit(solution)/shard_map/all_gather | solution.py:95
  64.7 368.7 %all-reduce.30.cloned.1.call-start = ((), (), s32[]{:S(2)}) async-start(), calls=%async_computation.9 | async-start | bytes 655360
  88.3 66.7 %copy-start.110 = (f32[640]{0:T(1024)}, f32[640]{0:T(1024)S(1)}, u32[]{:S(2)}) copy-start(f32[640]{0:T(1024)S(1)} %get-tuple-element.48) | copy-start | bytes 7684
  88.4 8.9 %copy-start.62 = (f32[1280]{0:T(1024)}, f32[1280]{0:T(1024)S(1)}, u32[]{:S(2)}) copy-start(f32[1280]{0:T(1024)S(1)} %get-tuple-element.46) | copy-start | bytes 15364
  88.4 8.9 %copy-start.92 = (f32[1280]{0:T(1024)}, f32[1280]{0:T(1024)S(1)}, u32[]{:S(2)}) copy-start(f32[1280]{0:T(1024)S(1)} %get-tuple-element.45) | copy-start | bytes 15364
  88.9 5.5 copy-start.114
  88.9 5.5 copy-start.115
  97.2 6.2 copy-start.74
  97.2 6.2 copy-start.88
  97.2 6.2 copy-start.90
  103.4 5.5 copy-start.33
  127.6 9.4 %copy-start.55 = (bf16[1024,3200]{1,0:T(8,128)(2,1)S(1)}, bf16[1024,3200]{1,0:T(8,128)(2,1)}, u32[]{:S(2)}) copy-start(bf16[1024,3200]{1,0:T(8,128)(2,1)} %copy-done.54) | copy-start | bytes 19660804
  127.6 9.4 %copy-start.118 = (bf16[3200,640]{0,1:T(8,128)(2,1)S(1)}, bf16[3200,640]{0,1:T(8,128)(2,1)}, u32[]{:S(2)}) copy-start(bf16[3200,640]{0,1:T(8,128)(2,1)} %all-gather.8.cloned.1.call-done) | copy-start | bytes 12288004
  137.0 5.6 copy-start.16
  142.6 12.4 %slice-start = ((s8[5242880]{0:T(1024)(128)(4,1)}), s8[1048576]{0:T(1024)(128)(4,1)S(1)}, s32[]{:S(2)}) async-start(s8[5242880]{0:T(1024)(128)(4,1)} %bitcast.119), calls=%async_computation.10 | async-start | bytes 2097152
  144.1 10.1 %copy-start.84 = (f32[1024]{0:T(1024)}, f32[1024]{0:T(1024)S(1)}, u32[]{:S(2)}) copy-start(f32[1024]{0:T(1024)S(1)} %get-tuple-element.68) | copy-start | bytes 12292
  144.1 10.1 %copy-start.86 = (f32[1024]{0:T(1024)}, f32[1024]{0:T(1024)S(1)}, u32[]{:S(2)}) copy-start(f32[1024]{0:T(1024)S(1)} %get-tuple-element.67) | copy-start | bytes 12292
  146.9 8.1 %slice-start.1 = ((s8[5242880]{0:T(1024)(128)(4,1)}), s8[4194304]{0:T(1024)(128)(4,1)S(1)}, s32[]{:S(2)}) async-start(s8[5242880]{0:T(1024)(128)(4,1)} %bitcast.119), calls=%async_computation.11 | async-start | bytes 8388608
  154.2 8.3 %copy-start.2 = (f32[1024,1280]{1,0:T(8,128)}, f32[1024,1280]{1,0:T(8,128)S(1)}, u32[]{:S(2)}) copy-start(f32[1024,1280]{1,0:T(8,128)S(1)} %get-tuple-element.222) | copy-start | bytes 15728644
  154.9 6.9 copy-start.68
  172.2 7.6 %copy-start.107 = (s32[128]{0:T(128)S(1)}, s32[128]{0:T(128)}, u32[]{:S(2)}) copy-start(s32[128]{0:T(128)} %get-tuple-element.208) | copy-start | bytes 1540
  172.2 7.6 %copy-start.109 = (f32[128]{0:T(128)S(1)}, f32[128]{0:T(128)}, u32[]{:S(2)}) copy-start(f32[128]{0:T(128)} %is-finite_select_fusion.1) | copy-start | bytes 1540
  184.7 13.3 %slice-start.6 = ((s8[5242880]{0:T(1024)(128)(4,1)}), s8[1048576]{0:T(1024)(128)(4,1)S(1)}, s32[]{:S(2)}) async-start(s8[5242880]{0:T(1024)(128)(4,1)} %bitcast.125), calls=%async_computation.16 | async-start | bytes 2097152
  189.1 8.8 %copy-start.71 = (f32[1024]{0:T(1024)S(1)}, f32[1024]{0:T(1024)}, u32[]{:S(2)}) copy-start(f32[1024]{0:T(1024)} %copy-done.70) | copy-start | bytes 12292
  189.1 8.9 %copy-start.69 = (f32[1024]{0:T(1024)S(1)}, f32[1024]{0:T(1024)}, u32[]{:S(2)}) copy-start(f32[1024]{0:T(1024)} %copy-done.68) | copy-start | bytes 12292
  189.1 8.9 %slice-start.7 = ((s8[5242880]{0:T(1024)(128)(4,1)}), s8[4194304]{0:T(1024)(128)(4,1)S(1)}, s32[]{:S(2)}) async-start(s8[5242880]{0:T(1024)(128)(4,1)} %bitcast.125), calls=%async_computation.17 | async-start | bytes 8388608
  189.1 9.8 %copy-start.8 = (f32[1024,1280]{1,0:T(8,128)S(1)}, f32[1024,1280]{1,0:T(8,128)}, u32[]{:S(2)}) copy-start(f32[1024,1280]{1,0:T(8,128)} %scatter_custom_fusion) | copy-start | bytes 15728644
  189.1 11.3 %copy-start.9 = (f32[1024,1280]{1,0:T(8,128)S(1)}, f32[1024,1280]{1,0:T(8,128)}, u32[]{:S(2)}) copy-start(f32[1024,1280]{1,0:T(8,128)} %scatter_custom_fusion.1) | copy-start | bytes 15728644
  219.6 6.0 copy-start.17
  219.6 6.0 copy-start.111
  225.6 6.3 copy-start.31
  225.6 6.3 copy-start.123
  235.2 6.1 copy-start.87
  235.2 6.2 copy-start.85
  247.3 7.4 %copy-start.119 = (bf16[3200,640]{0,1:T(8,128)(2,1)S(1)}, bf16[3200,640]{0,1:T(8,128)(2,1)}, u32[]{:S(2)}) copy-start(bf16[3200,640]{0,1:T(8,128)(2,1)} %all-gather.8.cloned.1.call-done) | copy-start | bytes 12288004
  260.1 8.0 %copy-start.19 = (f32[1024,3200]{1,0:T(8,128)}, f32[1024,3200]{1,0:T(8,128)S(1)}, u32[]{:S(2)}) copy-start(f32[1024,3200]{1,0:T(8,128)S(1)} %fusion.223) | copy-start | bytes 39321604
  260.1 8.0 %copy-start.36 = (bf16[1024,640]{1,0:T(8,128)(2,1)S(1)}, bf16[1024,640]{1,0:T(8,128)(2,1)}, u32[]{:S(2)}) copy-start(bf16[1024,640]{1,0:T(8,128)(2,1)} %get-tuple-element.170) | copy-start | bytes 3932164
  275.6 7.9 %copy-start.20 = (f32[1024,3200]{1,0:T(8,128)}, f32[1024,3200]{1,0:T(8,128)S(1)}, u32[]{:S(2)}) copy-start(f32[1024,3200]{1,0:T(8,128)S(1)} %fusion.225) | copy-start | bytes 39321604
  275.6 7.9 %copy-start.105 = (f32[1008]{0:T(1024)S(1)}, f32[1008]{0:T(1024)}, u32[]{:S(2)}) copy-start(f32[1008]{0:T(1024)} %slice.326) | copy-start | bytes 12100
  294.4 8.7 %copy-start.83 = (f32[1024]{0:T(1024)S(1)}, f32[1024]{0:T(1024)}, u32[]{:S(2)}) copy-start(f32[1024]{0:T(1024)} %copy-done.82) | copy-start | bytes 12292
  294.4 8.7 %copy-start.81 = (f32[1024]{0:T(1024)S(1)}, f32[1024]{0:T(1024)}, u32[]{:S(2)}) copy-start(f32[1024]{0:T(1024)} %copy-done.80) | copy-start | bytes 12292
  322.4 15.4 %slice-start.2 = ((s8[5242880]{0:T(1024)(128)(4,1)}), s8[4194304]{0:T(1024)(128)(4,1)S(1)}, s32[]{:S(2)}) async-start(s8[5242880]{0:T(1024)(128)(4,1)} %bitcast.121), calls=%async_computation.12 | async-start | bytes 8388608
  322.4 15.4 %slice-start.4 = ((s8[5242880]{0:T(1024)(128)(4,1)}), s8[4194304]{0:T(1024)(128)(4,1)S(1)}, s32[]{:S(2)}) async-start(s8[5242880]{0:T(1024)(128)(4,1)} %bitcast.123), calls=%async_computation.14 | async-start | bytes 8388608
  322.5 15.2 %copy-start.75 = (f32[1024]{0:T(1024)S(1)}, f32[1024]{0:T(1024)}, u32[]{:S(2)}) copy-start(f32[1024]{0:T(1024)} %copy-done.74) | copy-start | bytes 12292
  322.5 15.3 %copy-start.73 = (f32[1024]{0:T(1024)S(1)}, f32[1024]{0:T(1024)}, u32[]{:S(2)}) copy-start(f32[1024]{0:T(1024)} %copy-done.72) | copy-start | bytes 12292
  322.6 15.3 %slice-start.3 = ((s8[5242880]{0:T(1024)(128)(4,1)}), s8[1048576]{0:T(1024)(128)(4,1)S(1)}, s32[]{:S(2)}) async-start(s8[5242880]{0:T(1024)(128)(4,1)} %bitcast.121), calls=%async_computation.13 | async-start | bytes 2097152
  322.6 15.3 %slice-start.5 = ((s8[5242880]{0:T(1024)(128)(4,1)}), s8[1048576]{0:T(1024)(128)(4,1)S(1)}, s32[]{:S(2)}) async-start(s8[5242880]{0:T(1024)(128)(4,1)} %bitcast.123), calls=%async_computation.15 | async-start | bytes 2097152
  347.6 10.2 %slice-start.8 = ((s8[5242880]{0:T(1024)(128)(4,1)}), s8[1048576]{0:T(1024)(128)(4,1)S(1)}, s32[]{:S(2)}) async-start(s8[5242880]{0:T(1024)(128)(4,1)} %bitcast.127), calls=%async_computation.18 | async-start | bytes 2097152
  348.9 8.9 %slice-start.9 = ((s8[5242880]{0:T(1024)(128)(4,1)}), s8[4194304]{0:T(1024)(128)(4,1)S(1)}, s32[]{:S(2)}) async-start(s8[5242880]{0:T(1024)(128)(4,1)} %bitcast.127), calls=%async_computation.19 | async-start | bytes 8388608
  348.9 8.9 %copy-start.77 = (s32[1,1024]{1,0:T(1,128)S(1)}, s32[1,1024]{1,0:T(1,128)}, u32[]{:S(2)}) copy-start(s32[1,1024]{1,0:T(1,128)} %copy-done.76) | copy-start | bytes 12292
  357.9 7.3 %copy-start.32 = (f32[30,1280]{0,1:T(8,128)S(1)}, f32[30,1280]{0,1:T(8,128)}, u32[]{:S(2)}) copy-start(f32[30,1280]{0,1:T(8,128)} %fusion.111) | copy-start | bytes 460804
  370.2 7.6 %copy-start.15 = (f32[1024,640]{1,0:T(8,128)S(1)}, f32[1024,640]{1,0:T(8,128)}, u32[]{:S(2)}) copy-start(f32[1024,640]{1,0:T(8,128)} %copy-done.12) | copy-start | bytes 7864324
  377.5 91.6 %reduce-scatter.9.cloned.1.call-start = ((), (), s32[]{:S(2)}) async-start(), calls=%async_computation.8 | async-start | bytes 1843200 | tf_op jit(solution)/shard_map/reduce_scatter | solution.py:328
  384.4 119.6 %reduce-scatter.5.cloned.1.call-start = ((), (), s32[]{:S(2)}) async-start(), calls=%async_computation.6 | async-start | bytes 1843200 | tf_op jit(solution)/shard_map/reduce_scatter | solution.py:322
  392.6 8.3 %copy-start.37 = (bf16[1024,640]{1,0:T(8,128)(2,1)S(1)}, bf16[1024,640]{1,0:T(8,128)(2,1)}, u32[]{:S(2)}) copy-start(bf16[1024,640]{1,0:T(8,128)(2,1)} %get-tuple-element.170) | copy-start | bytes 3932164
  392.6 161.3 %reduce-scatter.7.cloned.1.call-start = ((), (), s32[]{:S(2)}) async-start(), calls=%async_computation.7 | async-start | bytes 4608000 | tf_op jit(solution)/shard_map/reduce_scatter | solution.py:325
  (78 other events, 238.3 us)
Sparse Core Ops, SparseCore 0:
  26.3 32.3 all-gather.5
  61.1 51.8 all-gather.7
  115.5 31.3 all-gather.9
  377.6 55.6 all-reduce.29
  435.5 33.4 reduce-scatter.8
  471.2 32.7 reduce-scatter.4
  506.3 47.5 reduce-scatter.6
where the time goes:
time: 709 us; the launch traced here: 702 us
  blocking collectives  184 us (26%)
  matrix products  151 us (21%)
  waiting for transfers between devices  135 us (19%)
  other arithmetic  119 us (17%)
  local copies, waits for them, and re-layouts  82.3 us (12%)
  between operations  30.3 us (4%)
    psum x1, blocking collectives, local(): lax.psum((in_rows, conv_rows, out_rows, vec_rows), 'dp')  67.4 us
    reduce_scatter x1, waiting for transfers between devices, local(): lax.psum_scatter(conv_sum.astype(jnp.bfloat16), 'fsdp', scatter_dimension...  49.9 us
    psum x1, blocking collectives, local(): lax.psum((summed_loss, slot_count, square_local), ('dp', 'fsdp'))  42.8 us
    reduce_scatter x1, waiting for transfers between devices, local(): lax.psum_scatter(in_sum.astype(jnp.bfloat16), 'fsdp', scatter_dimension=0...  34.9 us
    reduce_scatter x1, waiting for transfers between devices, local(): lax.psum_scatter(out_sum.astype(jnp.bfloat16), 'fsdp', scatter_dimension=...  34.9 us
    concatenate x18, local copies, waits for them, and re-layouts, backward(): vec_grad = jnp.concatenate([table_grad, head_grad, small_rows], axis=0)  31.4 us
    unnamed x274, local copies, waits for them, and re-layouts  30.5 us
    reduce_sum x4, other arithmetic, layer_norm(): return centre * lax.rsqrt(spread + norm_eps) * norm_gain + norm_bias  23.9 us
  transfers between devices with their start and end apart: 7, of which 5 were waited for; matrix products, arithmetic and copies ran while one was open for 14% of the time, Pallas kernels for 0%

commit v1 on v0

v1 whole, which is shorter than its diff:
```python
from functools import partial

import jax
import jax.numpy as jnp
from jax import lax
from jax.sharding import PartitionSpec as P

VOCAB = 30
CONV_TAPS = 5
DILATION = 8
TABLE = 32


beta_one = 0.9
beta_two = 0.95
epsilon = 1e-08
rate_matrix = 0.02
rate_vector = 0.5
decay_weight = 0.01
clip_limit = 0.02
norm_eps = 1e-05
highest_precision = lax.Precision.HIGHEST


def layer_norm(values, norm_gain, norm_bias):
    centre = values - jnp.mean(values, axis=-1, keepdims=True)
    spread = jnp.mean(centre * centre, axis=-1, keepdims=True)
    return centre * lax.rsqrt(spread + norm_eps) * norm_gain + norm_bias


def norm_gelu(values, norm_gain, norm_bias):
    return jax.nn.gelu(layer_norm(values, norm_gain, norm_bias), approximate=True)


def slot_loss(logits, labels, valid_slot):
    log_total = jax.nn.logsumexp(logits, axis=-1)
    hits = labels[:, None] == jnp.arange(logits.shape[1], dtype=jnp.int32)[None, :]
    chosen = jnp.sum(jnp.where(hits, logits, 0.0), axis=-1)
    return jnp.sum(jnp.where(valid_slot, log_total - chosen, 0.0))


def moved_groups(values, step):
    if step > 0:
        return jnp.concatenate([values[:, step:], jnp.full_like(values[:, :step], -1)], axis=1)
    if step < 0:
        return jnp.concatenate([jnp.full_like(values[:, :-step], -1), values[:, :step]], axis=1)
    return values


def tap_onehots(tokens, items, positions):
    batches, slots = positions.shape
    stride = tokens.shape[1] // slots
    token_groups = tokens.reshape(batches, slots, stride)
    item_groups = items.reshape(batches, slots, stride)
    valid = positions >= 0
    residue = jnp.where(valid, positions - stride * jnp.arange(slots, dtype=jnp.int32)[None], -1)
    chosen = residue[:, :, None] == jnp.arange(stride, dtype=jnp.int32)[None, None]
    own_item = jnp.sum(jnp.where(chosen, item_groups, 0), axis=2)
    identities = jnp.arange(TABLE, dtype=jnp.int32)
    result = []
    for tap in range(CONV_TAPS):
        step = (tap - CONV_TAPS // 2) * DILATION // stride
        item = jnp.sum(jnp.where(chosen, moved_groups(item_groups, step), 0), axis=2)
        token = jnp.sum(jnp.where(chosen, moved_groups(token_groups, step), 0), axis=2)
        keep = valid & (item == own_item) & (own_item >= 0)
        result.append(jnp.where(keep, token, -1)[:, :, None] == identities)
    return jnp.concatenate(result, axis=2).reshape(batches * slots, CONV_TAPS * TABLE)


def exact_dot(left, right, contract):
    high = left.astype(jnp.bfloat16)
    low = (left - high.astype(jnp.float32)).astype(jnp.bfloat16)
    return lax.dot_general(high, right, contract, preferred_element_type=jnp.float32) + lax.dot_general(
        low, right, contract, preferred_element_type=jnp.float32
    )


def column_sum(values):
    return jnp.sum(values, axis=0, dtype=jnp.float32)


def gathered_weights(shards):
    parted = (
        lax.all_gather(shards[0], "fsdp", axis=0, tiled=True),
        lax.all_gather(shards[1], "fsdp", axis=0, tiled=True),
        lax.all_gather(shards[2], "fsdp", axis=0, tiled=True),
        lax.all_gather(shards[3], "fsdp", axis=1, tiled=True),
    )
    return (
        lax.all_gather(parted[0], "dp", axis=1, tiled=True),
        lax.all_gather(parted[1], "dp", axis=1, tiled=True),
        lax.all_gather(parted[2], "dp", axis=1, tiled=True),
        lax.all_gather(parted[3], "dp", axis=1, tiled=True),
    )


def eigenbasis_update(
    gradient, master, moment, square, rotated_grads, col_start, first_correction, second_correction
):
    rotated = jnp.dot(gradient, rotated_grads, precision=highest_precision)
    moment_new = beta_one * moment + (1.0 - beta_one) * rotated
    square_new = beta_two * square + (1.0 - beta_two) * rotated * rotated
    step_ratio = (
        moment_new / first_correction / (jnp.sqrt(square_new / second_correction) + epsilon)
    )
    own_basis = lax.dynamic_slice_in_dim(rotated_grads, col_start, master.shape[1], 0)
    update = jnp.einsum("ri,ci->rc", step_ratio, own_basis, precision=highest_precision)
    master_new = master - rate_matrix * (update + decay_weight * master)
    return (master_new, master_new.astype(jnp.bfloat16), moment_new, square_new)


def adam_vectors(gradient, master, moment, square, first_correction, second_correction):
    decay_rows = jnp.where(
        jnp.arange(master.shape[0], dtype=jnp.int32)[:, None] < 2 * VOCAB, decay_weight, 0.0
    )
    moment_new = beta_one * moment + (1.0 - beta_one) * gradient
    square_new = beta_two * square + (1.0 - beta_two) * gradient * gradient
    step_ratio = (
        moment_new / first_correction / (jnp.sqrt(square_new / second_correction) + epsilon)
    )
    master_new = master - rate_vector * (step_ratio + decay_rows * master)
    return (master_new, master_new.astype(jnp.bfloat16), moment_new, square_new)


def local(
    input_tokens,
    item_numbers,
    loss_positions,
    target_tokens,
    input_projection,
    dilated_conv,
    output_projection,
    vectors,
    input_first_moment,
    input_second_moment,
    conv_first_moment,
    conv_second_moment,
    output_first_moment,
    output_second_moment,
    vector_first_moment,
    vector_second_moment,
    bases,
    eigenbasis_flags,
    optimizer_step,
):
    shards_low = (
        input_projection.astype(jnp.bfloat16),
        dilated_conv.astype(jnp.bfloat16),
        output_projection.astype(jnp.bfloat16),
        vectors.astype(jnp.bfloat16),
    )
    weight_in, weight_conv, weight_out, table_low = gathered_weights(shards_low)
    groups, col_index = lax.axis_size("dp"), lax.axis_index("dp")
    rows, row_index = lax.axis_size("fsdp"), lax.axis_index("fsdp")
    inner = weight_in.shape[1]
    width = weight_in.shape[0]
    start = 2 * VOCAB
    table = table_low.astype(jnp.float32)
    head = table_low[VOCAB:start]
    onehots = tap_onehots(input_tokens, item_numbers, loss_positions)
    onehots_low = onehots.astype(jnp.bfloat16)
    centre = CONV_TAPS // 2 * TABLE
    centre_low = onehots_low[:, centre : centre + TABLE]
    embedded = jnp.concatenate([table_low[:VOCAB], jnp.zeros((TABLE - VOCAB, width), jnp.bfloat16)], axis=0)
    first_act, first_back = jax.vjp(
        norm_gelu, embedded.astype(jnp.float32), table[start], table[start + 1]
    )
    first_low = first_act.astype(jnp.bfloat16)
    pre_inner = (
        jnp.dot(first_low, weight_in, preferred_element_type=jnp.float32)
        + table[start + 6, :inner]
    )
    second_act, second_back = jax.vjp(
        norm_gelu, pre_inner, table[start + 5, :inner], table[start + 5, inner:]
    )
    second_low = second_act.astype(jnp.bfloat16)
    picked_act = [
        jnp.dot(
            onehots_low[:, tap * TABLE : (tap + 1) * TABLE],
            second_low,
            preferred_element_type=jnp.float32,
        ).astype(jnp.bfloat16)
        for tap in range(CONV_TAPS)
    ]
    conv_input = (
        jnp.dot(
            jnp.concatenate(picked_act, axis=1), weight_conv, preferred_element_type=jnp.float32
        )
        + table[start + 6, inner:]
    )
    third_act, third_back = jax.vjp(
        norm_gelu, conv_input, table[start + 7, :inner], table[start + 7, inner:]
    )
    third_low = third_act.astype(jnp.bfloat16)
    branch = (
        jnp.einsum("ti,di->td", third_low, weight_out, preferred_element_type=jnp.float32)
        + table[start + 2]
    )
    picked_embedded = jnp.dot(centre_low, embedded, preferred_element_type=jnp.float32)
    final_out, final_back = jax.vjp(
        layer_norm, picked_embedded + branch, table[start + 3], table[start + 4]
    )
    picked = final_out.astype(jnp.bfloat16)
    logits = jnp.einsum("pd,vd->pv", picked, head, preferred_element_type=jnp.float32)
    valid = loss_positions.reshape(-1) >= 0
    summed_loss, loss_back = jax.vjp(
        partial(slot_loss, labels=target_tokens.reshape(-1), valid_slot=valid), logits
    )
    logit_grad = loss_back(jnp.ones((), jnp.float32))[0].astype(jnp.bfloat16)
    head_grad = jnp.einsum("pv,pd->vd", logit_grad, picked, preferred_element_type=jnp.float32)
    picked_grad = jnp.dot(logit_grad, head, preferred_element_type=jnp.float32)
    sum_grad, gain_four, bias_four = final_back(picked_grad)
    branch_low = sum_grad.astype(jnp.bfloat16)
    out_grad = jnp.einsum("td,ti->di", branch_low, third_low, preferred_element_type=jnp.float32)
    third_grad = jnp.dot(branch_low, weight_out, preferred_element_type=jnp.float32)
    conv_pre, gain_three, bias_three = third_back(third_grad)
    conv_low = conv_pre.astype(jnp.bfloat16)
    tap_grads = lax.dot_general(
        onehots_low, conv_low, (((0,), (0,)), ((), ())), preferred_element_type=jnp.float32
    )
    start_grads = jnp.einsum(
        "tv,td->vd", centre_low.astype(jnp.float32), sum_grad, precision=highest_precision
    )
    slot_count = jnp.sum(valid.astype(jnp.float32))
    wide_rows = jnp.concatenate(
        [
            start_grads[:VOCAB],
            head_grad,
            jnp.stack(
                [
                    column_sum(branch_low),
                    gain_four,
                    bias_four,
                    jnp.concatenate([gain_three, bias_three]),
                ]
            ),
        ],
        axis=0,
    )
    out_rows = lax.psum(
        lax.psum_scatter(out_grad.astype(jnp.bfloat16), "fsdp", scatter_dimension=0, tiled=True), "dp"
    ).astype(jnp.float32)
    tap_grads, wide_rows, summed_loss, slot_count = lax.psum(
        (tap_grads, wide_rows, summed_loss, slot_count), ("dp", "fsdp")
    )

    tap_view = tap_grads.reshape(CONV_TAPS, TABLE, inner)
    second_grad = sum(
        exact_dot(tap_view[tap], weight_conv[tap * inner : (tap + 1) * inner], (((1,), (1,)), ((), ())))
        for tap in range(CONV_TAPS)
    )
    inner_pre, gain_two, bias_two = second_back(second_grad)
    first_grad = exact_dot(inner_pre, weight_in, (((1,), (1,)), ((), ())))
    table_grad, gain_one, bias_one = first_back(first_grad)
    vec_sum = jnp.concatenate(
        [
            table_grad[:VOCAB] + wide_rows[:VOCAB],
            wide_rows[VOCAB:start],
            jnp.stack(
                [
                    gain_one,
                    bias_one,
                    wide_rows[start],
                    wide_rows[start + 1],
                    wide_rows[start + 2],
                    jnp.concatenate([gain_two, bias_two]),
                    jnp.concatenate(
                        [jnp.sum(inner_pre, axis=0), jnp.sum(tap_view[CONV_TAPS // 2], axis=0)]
                    ),
                    wide_rows[start + 3],
                ]
            ),
        ],
        axis=0,
    )
    own = width // (groups * rows)
    vec_own = lax.dynamic_slice_in_dim(vec_sum, (col_index * rows + row_index) * own, own, 1)

    row_low = lax.dynamic_slice_in_dim(first_low, row_index * (width // rows), width // rows, 1)
    in_rows = jnp.einsum(
        "vr,vi->ri", row_low.astype(jnp.float32), inner_pre, precision=highest_precision
    )
    placed = (
        jnp.eye(CONV_TAPS, dtype=jnp.bfloat16)[:, None, :, None] * second_low[None, :, None, :]
    ).reshape(CONV_TAPS * TABLE, CONV_TAPS * inner)
    conv_count = CONV_TAPS * inner // rows
    conv_low_rows = lax.dynamic_slice_in_dim(placed, row_index * conv_count, conv_count, 1)
    conv_rows = jnp.einsum(
        "vr,vi->ri", conv_low_rows.astype(jnp.float32), tap_grads, precision=highest_precision
    )

    col_width = input_projection.shape[1]
    col_start = col_index * col_width
    owned = [
        lax.dynamic_slice_in_dim(full_rows, col_start, col_width, 1)
        for full_rows in (in_rows, conv_rows, out_rows)
    ]
    square_local = sum((jnp.sum(piece * piece) for piece in owned)) + jnp.sum(vec_own * vec_own)
    square_total = lax.psum(square_local, ("dp", "fsdp"))
    grad_norm = jnp.sqrt(square_total) / slot_count
    factor = jnp.minimum(1.0, clip_limit / grad_norm) / slot_count
    step_value = optimizer_step[0].astype(jnp.float32)
    first_correction = 1.0 - beta_one**step_value
    second_correction = 1.0 - beta_two**step_value
    identity = jnp.eye(bases.shape[1], dtype=jnp.float32)
    rotated_grads = [
        jnp.where(eigenbasis_flags[mat_index] == 1, bases[mat_index], identity)
        for mat_index in range(3)
    ]
    master_in, copy_in, moment_in, square_in = eigenbasis_update(
        in_rows * factor,
        input_projection,
        input_first_moment,
        input_second_moment,
        rotated_grads[0],
        col_start,
        first_correction,
        second_correction,
    )
    updated_conv, conv_bfloat_copy, updated_conv_moment, updated_conv_square = eigenbasis_update(
        conv_rows * factor,
        dilated_conv,
        conv_first_moment,
        conv_second_moment,
        rotated_grads[1],
        col_start,
        first_correction,
        second_correction,
    )
    master_out, copy_out, moment_out, square_out = eigenbasis_update(
        out_rows * factor,
        output_projection,
        output_first_moment,
        output_second_moment,
        rotated_grads[2],
        col_start,
        first_correction,
        second_correction,
    )
    master_vec, copy_vec, moment_vec, square_vec = adam_vectors(
        vec_own * factor,
        vectors,
        vector_first_moment,
        vector_second_moment,
        first_correction,
        second_correction,
    )
    return (
        summed_loss / slot_count,
        grad_norm,
        master_in,
        copy_in,
        moment_in,
        square_in,
        updated_conv,
        conv_bfloat_copy,
        updated_conv_moment,
        updated_conv_square,
        master_out,
        copy_out,
        moment_out,
        square_out,
        master_vec,
        copy_vec,
        moment_vec,
        square_vec,
    )


def solution(mesh):
    placed = (
        P(None, ("dp", "fsdp")),
        P(None, ("dp", "fsdp")),
        P(None, ("dp", "fsdp")),
        P(None, ("dp", "fsdp")),
        P("fsdp", "dp"),
        P("fsdp", "dp"),
        P("fsdp", "dp"),
        P(None, ("dp", "fsdp")),
        P("fsdp", None),
        P("fsdp", None),
        P("fsdp", None),
        P("fsdp", None),
        P("fsdp", None),
        P("fsdp", None),
        P(None, ("dp", "fsdp")),
        P(None, ("dp", "fsdp")),
        P(),
        P(),
        P(),
    )
    return jax.shard_map(
        local,
        mesh=mesh,
        in_specs=placed,
        out_specs=(
            P(),
            P(),
            P("fsdp", "dp"),
            P("fsdp", "dp"),
            P("fsdp", None),
            P("fsdp", None),
            P("fsdp", "dp"),
            P("fsdp", "dp"),
            P("fsdp", None),
            P("fsdp", None),
            P("fsdp", "dp"),
            P("fsdp", "dp"),
            P("fsdp", None),
            P("fsdp", None),
            P(None, ("dp", "fsdp")),
            P(None, ("dp", "fsdp")),
            P(None, ("dp", "fsdp")),
            P(None, ("dp", "fsdp")),
        ),
        check_vma=False,
    )
```

time: 709 us -> 454 us (0.64)
  matrix products: 151 us -> 46.7 us
  other arithmetic: 119 us -> 18.8 us
  waiting for transfers between devices: 135 us -> 208 us
  blocking collectives: 184 us -> 114 us
  local copies, waits for them, and re-layouts: 82.3 us -> 34.3 us
    psum x0 -> x2, waiting for transfers between devices: none -> 161 us  [the longest x1 127 us: local(): lax.psum((tap_grads, wide_rows, summed_loss, slot_count), ('dp', 'fsdp'))]
    reduce_scatter x3 -> x1, waiting for transfers between devices: 120 us -> 16.4 us  [local(): lax.psum_scatter(out_grad.astype(jnp.bfloat16), 'fsdp', scatter_dimension...]
    dot_general x24 -> x30, matrix products: 117 us -> 33.8 us  [the longest x5 5.32 us: local(): jnp.dot(onehots_low[:, tap * TABLE:(tap + 1) * TABLE], second_low, prefer...]
    psum x2 -> x1, blocking collectives: 110 us -> 40 us  [local(): lax.psum((tap_grads, wide_rows, summed_loss, slot_count), ('dp', 'fsdp'))]
    all_gather x1, waiting for transfers between devices: 2.78 us -> 29.3 us  [gathered_weights(): lax.all_gather(parted[2], 'dp', axis=1, tiled=True)]
    unnamed x274 -> x93, local copies, waits for them, and re-layouts: 30.5 us -> 4.79 us
    reduce_sum x6 -> x4, other arithmetic: 25.9 us -> 1.23 us  [the longest x1 0.61 us: local(): slot_count = jnp.sum(valid.astype(jnp.float32))]
    concatenate x18 -> x3, local copies, waits for them, and re-layouts: 31.4 us -> 9.6 us  [the longest x1 4.82 us: local(): jnp.concatenate([table_grad[:VOCAB] + wide_rows[:VOCAB], wide_rows[VOCAB:...]
  transfers between devices with their start and end apart: 7 -> 6, of which waited for: 5 -> 5; matrix products, arithmetic and copies ran while one was open for 14% -> 14% of each run, Pallas kernels for 0% -> 0%
where the time goes in v1:
time: 454 us; the launch traced here: 449 us
  waiting for transfers between devices  208 us (46%)
  blocking collectives  114 us (25%)
  matrix products  46.7 us (10%)
  local copies, waits for them, and re-layouts  34.3 us (8%)
  between operations  27.2 us (6%)
  other arithmetic  18.8 us (4%)
    psum x1, waiting for transfers between devices, local(): lax.psum((tap_grads, wide_rows, summed_loss, slot_count), ('dp', 'fsdp'))  127 us
    psum x1, blocking collectives, local(): lax.psum((tap_grads, wide_rows, summed_loss, slot_count), ('dp', 'fsdp'))  40 us
    psum x1, waiting for transfers between devices, local(): lax.psum(lax.psum_scatter(out_grad.astype(jnp.bfloat16), 'fsdp', scatter_...  33.9 us
    all_gather x1, waiting for transfers between devices, gathered_weights(): lax.all_gather(parted[2], 'dp', axis=1, tiled=True)  29.3 us
    all_gather x1, blocking collectives, gathered_weights(): lax.all_gather(shards[1], 'fsdp', axis=0, tiled=True)  19 us
    all_gather x1, blocking collectives, gathered_weights(): lax.all_gather(shards[0], 'fsdp', axis=0, tiled=True)  17 us
    reduce_scatter x1, waiting for transfers between devices, local(): lax.psum_scatter(out_grad.astype(jnp.bfloat16), 'fsdp', scatter_dimension...  16.4 us
    all_gather x1, blocking collectives, gathered_weights(): lax.all_gather(shards[2], 'fsdp', axis=0, tiled=True)  15.1 us
  transfers between devices with their start and end apart: 6, of which 5 were waited for; matrix products, arithmetic and copies ran while one was open for 14% of the time, Pallas kernels for 0%

profile of v1, /device:TPU:0, one launch (start us, length us, event | category | flops | bytes accessed | tf_op | source)
XLA Modules:
  0.0 448.9 jit_solution(13318790857752670244)
XLA Ops:
  7.2 1.0 convert_element_type.159
  8.2 17.0 %all_gather.26 = bf16[1280,160]{1,0:T(8,128)(2,1)S(1)} all-gather(bf16[160,160]{1,0:T(8,128)(2,1)S(1)} %convert_element_type.159), channel_id=1, replica_groups=mesh['dp'=4,'fsdp'=8] {'fsdp'}, dimensions={0}, use_global_device_ids=true | all-gather | bytes 460800 | tf_op jit(solution)/shard_map/all_gather | solution.py:84
  25.2 1.0 copy.93
  26.2 19.0 %all-gather.1 = bf16[8,400,160]{1,2,0:T(8,128)(2,1)S(1)} all-gather(bf16[1,400,160]{1,2,0:T(8,128)(2,1)S(1)} %convert_bitcast_fusion), channel_id=1, replica_groups=mesh['dp'=4,'fsdp'=8] {'fsdp'}, dimensions={0}, use_global_device_ids=true | all-gather | bytes 1152000 | tf_op jit(solution)/shard_map/all_gather | solution.py:85
  45.3 0.7 copy.94
  46.0 2.4 reshape.268
  48.5 15.1 %all_gather.30 = bf16[1280,160]{1,0:T(8,128)(2,1)S(1)} all-gather(bf16[160,160]{1,0:T(8,128)(2,1)S(1)} %convert_element_type.168), channel_id=1, replica_groups=mesh['dp'=4,'fsdp'=8] {'fsdp'}, dimensions={0}, use_global_device_ids=true | all-gather | bytes 460800 | tf_op jit(solution)/shard_map/all_gather | solution.py:86
  63.7 1.0 copy.95
  65.4 13.9 %all_gather.24 = bf16[68,320]{0,1:T(8,128)(2,1)S(1)} all-gather(bf16[68,40]{0,1:T(8,128)(2,1)S(1)} %convert_element_type.155), channel_id=1, replica_groups=mesh['dp'=4,'fsdp'=8] {'fsdp'}, dimensions={1}, use_global_device_ids=true | all-gather | bytes 48960 | tf_op jit(solution)/shard_map/all_gather | solution.py:87
  79.4 9.0 %all-gather = bf16[4,320,68]{1,2,0:T(8,128)(2,1)S(1)} all-gather(bf16[1,320,68]{1,2,0:T(8,128)(2,1)S(1)} %copy.91), channel_id=1, replica_groups=mesh['dp'=4,'fsdp'=8] {'dp'}, dimensions={0}, use_global_device_ids=true | all-gather | bytes 217600 | tf_op jit(solution)/shard_map/all_gather | solution.py:93
  88.7 1.8 slice_reduce_fusion.1
  90.6 1.1 slice_reduce_fusion.6
  97.9 4.6 %convert_select_fusion = (f32[640,640]{1,0:T(8,128)}, f32[640,640]{1,0:T(8,128)}, f32[640,640]{1,0:T(8,128)S(1)}) fusion(f32[3,640,640]{2,1,0:T(8,128)} %param.35, pred[]{:T(512)} %bitcast.22, pred[]{:T(512)} %bitcast.16, pred[]{:T(512)} %bitcast.20), kind=kLoop, calls=%fused_computation.1 | loop fusion | flops 2048000 | bytes 9830403 | tf_op jit(solution)/shard_map/jit(_where)/select_n | solution.py:307
  102.8 2.2 fusion.164
  105.5 1.1 copy.112
  106.6 1.1 fusion.6
  107.7 1.1 fusion.5
  108.8 1.0 fusion.4
  109.8 1.1 fusion.3
  110.9 1.1 fusion.2
  111.9 1.0 all-gather.8.cloned.1.call-done
  112.9 4.3 fusion.165
  117.4 29.3 %all-gather.10.cloned.1.call-done = bf16[1280,640]{0,1:T(8,128)(2,1)} async-done(((bf16[1280,160]{0,1:T(8,128)(2,1)}), bf16[1280,640]{0,1:T(8,128)(2,1)}) %all-gather.10.cloned.1.call-update) | async-done | bytes 1638416 | tf_op jit(solution)/shard_map/all_gather | solution.py:92
  146.7 2.3 convolution_add_fusion.1
  150.8 0.8 multiply_reduce_fusion
  152.7 1.5 fusion
  154.4 1.1 multiply_reduce_fusion.3
  155.5 1.1 stack.21
  156.6 1.1 stack.20
  157.8 1.1 reshape.269
  158.8 1.1 reshape.270
  160.3 1.1 fusion.91
  161.3 4.6 %concatenate.62 = f32[64,1280]{0,1:T(8,128)} concatenate(f32[30,1280]{0,1:T(8,128)S(1)} %fusion, f32[30,1280]{0,1:T(8,128)S(1)} %fusion.150, f32[1,1280]{0,1:T(8,128)} %stack.20, f32[1,1280]{0,1:T(8,128)} %reshape.269, f32[1,1280]{0,1:T(8,128)} %reshape.270, f32[1,1280]{0,1:T(8,128)} %stack.21), dimensions={0} | concatenate | bytes 655360 | tf_op jit(solution)/shard_map/concatenate | solution.py:225
  166.6 3.4 convolution_convert_fusion
  170.1 126.9 %all-reduce.15.cloned.1.call-done = (f32[160,640]{1,0:T(8,128)}, f32[64,1280]{0,1:T(8,128)}) async-done(((f32[160,640]{1,0:T(8,128)}, f32[64,1280]{0,1:T(8,128)}), (f32[160,640]{1,0:T(8,128)}, f32[64,1280]{0,1:T(8,128)})) %all-reduce.15.cloned.1.call-update) | async-done | bytes 737296 | tf_op jit(solution)/shard_map/psum | solution.py:243
  296.9 2.3 slice.225
  299.2 2.2 slice.226
  301.4 1.4 fusion.32
  302.8 1.4 fusion.35
  306.9 1.1 stack.23
  308.0 1.1 stack.22
  309.1 0.8 fusion.121
  309.9 1.8 fusion.55
  311.7 1.1 reshape.271
  312.7 1.1 reshape.272
  313.9 1.1 fusion.117
  315.0 0.7 multiply_reduce_fusion.8
  316.1 1.3 fusion.158
  317.4 16.4 %reduce-scatter.2.cloned.1.call-done = bf16[160,640]{1,0:T(8,128)(2,1)} async-done(((bf16[1280,640]{1,0:T(8,128)(2,1)}), bf16[160,640]{1,0:T(8,128)(2,1)}) %reduce-scatter.2.cloned.1.call-update) | async-done | bytes 204816 | tf_op jit(solution)/shard_map/reduce_scatter | solution.py:241
  333.8 1.7 fusion.105
  335.5 0.8 multiply_reduce_fusion.6
  337.6 4.8 %concatenate.65 = f32[68,1280]{0,1:T(8,128)} concatenate(f32[30,1280]{0,1:T(8,128)} %get-tuple-element.155, f32[30,1280]{0,1:T(8,128)} %get-tuple-element.154, f32[1,1280]{0,1:T(8,128)} %reshape.271, f32[1,1280]{0,1:T(8,128)} %reshape.272, f32[3,1280]{0,1:T(8,128)} %slice.225, f32[1,1280]{0,1:T(8,128)} %stack.22, f32[1,1280]{0,1:T(8,128)} %stack.23, f32[1,1280]{0,1:T(8,128)} %slice.226), dimensions={0} | concatenate | bytes 696320 | tf_op jit(solution)/shard_map/concatenate | solution.py:255
  342.4 1.3 multiply_reduce_fusion.12
  343.7 33.9 %all-reduce.13.cloned.1.call-done = bf16[160,640]{1,0:T(8,128)(2,1)} async-done(((bf16[160,640]{1,0:T(8,128)(2,1)}), bf16[160,640]{1,0:T(8,128)(2,1)}) %all-reduce.13.cloned.1.call-update) | async-done | bytes 204816 | tf_op jit(solution)/shard_map/psum | solution.py:240
  377.7 1.0 convert_element_type.191
  378.6 0.7 multiply_reduce_fusion.7
  380.7 40.0 %all-reduce.8 = (f32[]{:T(128)}, f32[]{:T(128)}, f32[]{:T(128)}) all-reduce(f32[]{:T(128)} %get-tuple-element.126, f32[]{:T(128)} %get-tuple-element.125, f32[]{:T(128)S(6)} %add.335), channel_id=1, replica_groups=mesh['dp'=4,'fsdp'=8] {'dp','fsdp'}, use_global_device_ids=true, to_apply=%region_22.23 | all-reduce | flops 3 | bytes 24 | tf_op jit(solution)/shard_map/psum | solution.py:243
  424.8 4.8 %fusion.17 = (f32[400,640]{1,0:T(8,128)S(1)}, f32[400,640]{1,0:T(8,128)S(1)}) fusion(f32[400,640]{1,0:T(8,128)} %param.30, f32[400,640]{1,0:T(8,128)} %param.29, f32[640,640]{1,0:T(8,128)S(1)} %get-tuple-element.151, f32[400,640]{1,0:T(8,128)S(1)} %fusion.105, f32[]{:T(128)S(6)} %div.159), kind=kOutput, calls=%fused_computation.48 | convolution fusion | flops 1968128000 | bytes 6758404 | tf_op jit(solution)/shard_map/dot_general | solution.py:100
  429.7 1.4 fusion.73
  431.2 1.4 fusion.170
  432.6 2.4 fusion.169
  435.1 1.4 fusion.72
  436.5 1.4 fusion.168
  438.0 1.4 fusion.151
  (177 shorter events, 12.7 us)
Async XLA Ops:
  7.2 19.0 %copy-start.23 = (f32[400,160]{0,1:T(8,128)S(1)}, f32[400,160]{0,1:T(8,128)}, u32[]{:S(2)}) copy-start(f32[400,160]{0,1:T(8,128)} %param.24) | copy-start | bytes 768004
  7.2 95.5 %all-gather.6.cloned.1.call-start = ((), (), s32[]{:S(2)}) async-start(), calls=%async_computation.1 | async-start | bytes 2048000 | tf_op jit(solution)/shard_map/all_gather | solution.py:90
  26.2 86.8 %all-gather.8.cloned.1.call-start = ((), (), s32[]{:S(2)}) async-start(), calls=%async_computation.2 | async-start | bytes 5120000 | tf_op jit(solution)/shard_map/all_gather | solution.py:91
  46.0 2.5 copy-start.25
  48.4 16.3 %copy-start.33 = (s32[2,1024]{1,0:T(2,128)S(1)}, s32[2,1024]{1,0:T(2,128)}, u32[]{:S(2)}) copy-start(s32[2,1024]{1,0:T(2,128)} %param.20) | copy-start | bytes 24580
  48.4 16.4 %copy-start.34 = (s32[2,1024]{1,0:T(2,128)S(1)}, s32[2,1024]{1,0:T(2,128)}, u32[]{:S(2)}) copy-start(s32[2,1024]{1,0:T(2,128)} %param.19) | copy-start | bytes 24580
  48.5 98.3 %all-gather.10.cloned.1.call-start = ((), (), s32[]{:S(2)}) async-start(), calls=%async_computation.3 | async-start | bytes 2048000 | tf_op jit(solution)/shard_map/all_gather | solution.py:92
  64.6 0.7 copy-start.28
  64.6 232.3 %all-reduce.15.cloned.1.call-start = ((), (), s32[]{:S(2)}) async-start(), calls=%async_computation.6 | async-start | bytes 2129920 | tf_op jit(solution)/shard_map/psum | solution.py:243
  90.5 1.7 copy-start.36
  90.5 1.7 copy-start.31
  90.5 4.4 copy-start.35
  92.6 0.5 copy-start.40
  97.9 4.8 %copy-start.10 = (bf16[32,1280]{0,1:T(8,128)(2,1)}, bf16[32,1280]{0,1:T(8,128)(2,1)S(1)}, u32[]{:S(2)}) copy-start(bf16[32,1280]{0,1:T(8,128)(2,1)S(1)} %fusion.52) | copy-start | bytes 245764
  105.1 1.5 copy-start.42
  105.2 1.5 copy-start.37
  117.2 31.9 %copy-start.6 = (f32[256,640]{1,0:T(8,128)}, f32[256,640]{1,0:T(8,128)S(1)}, u32[]{:S(2)}) copy-start(f32[256,640]{1,0:T(8,128)S(1)} %get-tuple-element.179) | copy-start | bytes 1966084
  149.9 0.9 copy-start.32
  152.5 1.8 copy-start.7
  152.5 1.9 copy-start.44
  152.7 2.8 copy-start.14
  165.9 167.8 %reduce-scatter.2.cloned.1.call-start = ((), (), s32[]{:S(2)}) async-start(), calls=%async_computation.4 | async-start | bytes 1843200 | tf_op jit(solution)/shard_map/reduce_scatter | solution.py:241
  170.0 207.7 %all-reduce.13.cloned.1.call-start = ((), (), s32[]{:S(2)}) async-start(), calls=%async_computation.5 | async-start | bytes 409600 | tf_op jit(solution)/shard_map/psum | solution.py:240
  296.9 4.5 copy-start.5
  296.9 7.3 %copy-start = (bf16[3200,640]{0,1:T(8,128)(2,1)S(1)}, bf16[3200,640]{0,1:T(8,128)(2,1)}, u32[]{:S(2)}) copy-start(bf16[3200,640]{0,1:T(8,128)(2,1)} %all-gather.8.cloned.1.call-done) | copy-start | bytes 12288004
  305.3 0.8 copy-start.38
  305.8 0.7 copy-start.43
  306.1 3.0 copy-start.2
  311.7 4.1 copy-start.41
  312.7 3.3 copy-start.1
  315.0 0.8 copy-start.8
  424.8 4.9 %copy-start.3 = (f32[640,640]{1,0:T(8,128)S(1)}, f32[640,640]{1,0:T(8,128)}, u32[]{:S(2)}) copy-start(f32[640,640]{1,0:T(8,128)} %get-tuple-element.149) | copy-start | bytes 4915204
  424.8 4.9 %copy-start.13 = (bf16[160,640]{1,0:T(8,128)(2,1)S(1)}, bf16[160,640]{1,0:T(8,128)(2,1)}, u32[]{:S(2)}) copy-start(bf16[160,640]{1,0:T(8,128)(2,1)} %all-reduce.13.cloned.1.call-done) | copy-start | bytes 614404
  424.8 4.9 %copy-start.15 = (f32[160,640]{1,0:T(8,128)S(1)}, f32[160,640]{1,0:T(8,128)}, u32[]{:S(2)}) copy-start(f32[160,640]{1,0:T(8,128)} %param.32) | copy-start | bytes 1228804
  424.8 4.9 %copy-start.16 = (f32[160,640]{1,0:T(8,128)S(1)}, f32[160,640]{1,0:T(8,128)}, u32[]{:S(2)}) copy-start(f32[160,640]{1,0:T(8,128)} %param.31) | copy-start | bytes 1228804
  429.6 3.0 copy-start.11
  429.6 3.0 copy-start.12
  429.7 1.5 copy-start.26
  431.1 1.5 copy-start.19
  431.1 1.5 copy-start.20
  431.1 1.4 copy-start.24
  432.6 2.4 copy-start.4
  432.6 2.4 copy-start.9
  432.6 2.4 copy-start.17
  432.6 2.4 copy-start.18
  435.1 1.4 copy-start.27
  436.5 1.5 copy-start.21
  436.5 1.5 copy-start.22
  436.5 1.5 copy-start.29
  436.5 1.5 copy-start.30
  436.5 1.5 copy-start.39
Sparse Core Ops, SparseCore 0:
  26.3 32.3 all-gather.5
  61.1 51.7 all-gather.7
  115.3 31.3 all-gather.9
  166.0 130.8 all-reduce.14
  299.1 34.6 reduce-scatter.1
  336.5 41.0 all-reduce.12
